TPU v7x, 256 devices: a whole 4x4x8 slice. The times are simulated.
256 devices in a mesh: lat: 32 (over z, x_hi, core), lon: 8 (over y, x_lo).
Axes of the slice: x: 4 (x_hi: 2, x_lo: 2; x = x_hi * 2 + x_lo), y: 4, z: 8, core: 2. Of those that a mesh axis runs over, the one named last changes fastest.
Arguments:
- elevation: float32 [8192, 16384], P('lat', 'lon'), may hold values from -200 to 200
Outputs:
- slope_angle: float32 [8192, 16384], P('lat', 'lon')
- facing: float32 [2, 8192, 16384], P(None, 'lat', 'lon')
- hillshade: float32 [8192, 16384], P('lat', 'lon')
All inputs are finite; a program needn't handle non-finite values.
Results may differ from a plain program's by a relative error of at most 0.0003.
Values sent between devices are 32-bit elements; how exact they have to be, the bound alone decides.
A program may use at most 64 MiB of HBM per device.

v0:
```python
import math

import jax
import jax.numpy as jnp
from jax import lax
from jax.experimental import pallas as pl
from jax.experimental.pallas import tpu as pltpu
from jax.sharding import PartitionSpec as P

HALO = 64
LAGS = (1, 2, 4, 8, 16, 32, 64)
F32 = jnp.float32
ROWS, COLS, TILES = 256, 2048, 16


def pad_of(s):
    return max(8, s)


def shade(east, north, east_scale):
    grad_east = east * east_scale
    grad_north = north * (1.0 / 56.0)
    squared = grad_east * grad_east + grad_north * grad_north
    inverse = lax.rsqrt(1.0 + squared)
    a = jnp.sqrt(squared) * inverse
    b = 1.0 + inverse
    upper = a > 0.41421356 * b
    v = jnp.where(upper, a - b, a) / jnp.where(upper, a + b, b)
    z = v * v
    poly = ((8.05374449538e-2 * z - 1.38776856032e-1) * z + 1.99777106478e-1) * z - 3.33329491539e-1
    slope = 2.0 * (poly * z * v + v + jnp.where(upper, math.pi / 4, 0.0))
    facing_east = -grad_east * inverse
    facing_north = -grad_north * inverse
    shading = jnp.maximum(0.5 * (facing_north - facing_east) + math.sqrt(0.5) * inverse, 0.0)
    return slope, facing_east, facing_north, shading


def differences(z, lags):
    lane = lax.broadcasted_iota(jnp.int32, (8, 128), 1)
    out = {}
    for s in lags:
        right = [pltpu.roll(t, s, 1) for t in z[:-1]]
        if s == 64:
            left = [pltpu.roll(z[-1], 64, 1)]
            left = right[1:] + left
        else:
            left = [pltpu.roll(t, 128 - s, 1) for t in z[1:]]
        p, q = [], []
        for j in range(len(z) - 2):
            west = jnp.where(lane < s, right[j], right[j + 1])
            east = jnp.where(lane < 128 - s, left[j], left[j + 1])
            p.append((east - west) * (1.0 / s))
            q.append((east + west + 2.0 * z[j + 1]) * (1.0 / s))
        out[s] = (p, q)
    return out


CHUNK = 4
CHUNKS = TILES // CHUNK
SPANS = ((0, 5), (5, 4), (9, 4), (13, 3))


def exchange_kernel(
    x, scales, o_s, o_f, o_h, gs, zc, hz, packed, arrived, ps, qs, cs, en, pt, qt, sem_in, sem_out, sem_got, sem_gs
):
    lat, lon = lax.axis_index("lat"), lax.axis_index("lon")
    n_lat, n_lon = lax.axis_size("lat"), lax.axis_size("lon")
    east, west = lax.rem(lon + 1, n_lon), lax.rem(lon + n_lon - 1, n_lon)
    has_north, has_south = lat > 0, lat < n_lat - 1

    def load(k, j):
        return pltpu.make_async_copy(
            x.at[pl.ds(64 * k, 64), pl.ds(128 * j, 128)], zc.at[j + 1, pl.ds(64 * k, 64)], sem_in.at[k, j]
        )

    edges = [load(k, j) for j in (0, TILES - 1) for k in range(4)]
    rims = [load(k, j) for k in (0, 3) for j in range(1, TILES - 1)]
    middle = [load(k, j) for k in (1, 2) for j in range(1, TILES - 1)]
    for c in edges + rims + middle:
        c.start()
    scale_copy = pltpu.make_async_copy(scales, gs, sem_gs)
    scale_copy.start()

    barrier = pltpu.get_barrier_semaphore()

    def greet(to_lat, to_lon):
        pl.semaphore_signal(
            barrier, inc=1, device_id={"lat": to_lat, "lon": to_lon}, device_id_type=pl.DeviceIdType.MESH
        )

    greet(lat, east)
    greet(lat, west)

    @pl.when(has_north)
    def _():
        for to in (lon, east, west):
            greet(lat - 1, to)

    @pl.when(has_south)
    def _():
        for to in (lon, east, west):
            greet(lat + 1, to)

    lane = lax.broadcasted_iota(jnp.int32, (128, 128), 1)
    for c in edges:
        c.wait()
    packed[0] = jnp.where(lane < 64, pltpu.roll(zc[16, 0:128, :], 64, 1), zc[16, 128:256, :])
    packed[1] = jnp.where(lane < 64, zc[1, 0:128, :], pltpu.roll(zc[1, 128:256, :], 64, 1))
    for c in rims:
        c.wait()

    def send(src, dst, k, to_lat, to_lon):
        return pltpu.make_async_remote_copy(
            src_ref=src,
            dst_ref=dst,
            send_sem=sem_out.at[k],
            recv_sem=sem_got.at[k],
            device_id={"lat": to_lat, "lon": to_lon},
            device_id_type=pl.DeviceIdType.MESH,
        )

    first_rows, last_rows = pl.ds(0, 64), pl.ds(192, 64)
    along = [send(packed.at[0], arrived.at[0], 0, lat, east), send(packed.at[1], arrived.at[1], 1, lat, west)]
    south = [
        send(zc.at[16, last_rows], hz.at[0, 0], 2, lat + 1, east),
        send(zc.at[1, last_rows], hz.at[0, 17], 3, lat + 1, west),
    ]
    north = [
        send(zc.at[16, first_rows], hz.at[1, 0], 4, lat - 1, east),
        send(zc.at[1, first_rows], hz.at[1, 17], 5, lat - 1, west),
    ]
    for k, (at, n) in enumerate(SPANS):
        tiles = pl.ds(1 + at, n)
        south.append(send(zc.at[tiles, last_rows], hz.at[0, tiles], 6 + k, lat + 1, lon))
        north.append(send(zc.at[tiles, first_rows], hz.at[1, tiles], 10 + k, lat - 1, lon))

    inside = jnp.logical_and(has_north, has_south)
    pl.semaphore_wait(barrier, jnp.where(inside, 8, 5))
    for c in along:
        c.start()

    @pl.when(has_south)
    def _():
        for c in south:
            c.start()

    @pl.when(has_north)
    def _():
        for c in north:
            c.start()

    for k, s in enumerate(LAGS):
        m = pad_of(s)
        for ref in (ps[k], qs[k]):
            ref[:, 0:m, :] = jnp.zeros((TILES, m, 128), F32)
            ref[:, m + ROWS : m + ROWS + m, :] = jnp.zeros((TILES, m, 128), F32)
    zero = jnp.zeros((CHUNK, 8, 128), F32)
    for k in range(3):
        for ref in (pt[k], qt[k]):
            ref[0, :, 8:16, :] = zero
            ref[1, :, 0:8, :] = zero
    for c in middle:
        c.wait()
    scale_copy.wait()
    for c in along:
        c.wait()
    zc[0, 0:128, :] = pltpu.roll(arrived[0], 64, 1)
    zc[0, 128:256, :] = arrived[0]
    zc[17, 0:128, :] = arrived[1]
    zc[17, 128:256, :] = pltpu.roll(arrived[1], 64, 1)

    def first(row):
        z = [zc[j, pl.ds(row, 8), :] for j in range(TILES + 2)]
        d = differences(z, LAGS)
        for k, s in enumerate(LAGS):
            for j in range(TILES):
                ps[k][j, pl.ds(row + pad_of(s), 8), :] = d[s][0][j]
                qs[k][j, pl.ds(row + pad_of(s), 8), :] = d[s][1][j]
        for j in range(TILES):
            cs[j, pl.ds(row, 8), :] = 2.0 * sum(d[s][0][j] for s in LAGS)

    def second(row, j):
        to_east = cs[j, pl.ds(row, 8), :]
        to_north = None
        for k, s in enumerate(LAGS):
            m = pad_of(s)
            above, below = pl.ds(row + (m - s), 8), pl.ds(row + (m + s), 8)
            to_east = to_east + (ps[k][j, above, :] + ps[k][j, below, :])
            diff = qs[k][j, above, :] - qs[k][j, below, :]
            to_north = diff if to_north is None else to_north + diff
        return to_east, to_north

    def partial(row, side, to):
        for j in range(TILES):
            to_east, to_north = second(row, j)
            en[side, 0, j, pl.ds(to, 8), :] = to_east
            en[side, 1, j, pl.ds(to, 8), :] = to_north

    def put(rows, columns, values):
        o_s[rows, columns] = values[0]
        o_f[0, rows, columns] = values[1]
        o_f[1, rows, columns] = values[2]
        o_h[rows, columns] = values[3]

    def loop(lo, hi, body):
        def step(i, carry):
            body(pl.multiple_of(8 * i, 8))
            return carry

        lax.fori_loop(lo, hi, step, 0)

    def with_top(row):
        first(row)
        partial(pl.multiple_of(row - 64, 8), 0, pl.multiple_of(row - 64, 8))

    def with_middle(row):
        first(row)
        here = pl.multiple_of(row - 64, 8)
        scale = gs[pl.ds(here, 8), :]
        for j in range(TILES):
            put(pl.ds(here, 8), pl.ds(128 * j, 128), shade(*second(here, j), scale))

    loop(0, 8, first)
    loop(8, 16, with_top)
    loop(16, 32, with_middle)
    loop(24, 32, lambda row: partial(row, 1, pl.multiple_of(row - 192, 8)))

    def clamp(side):
        row = 0 if side == 0 else ROWS - 1
        for j in range(TILES + 2):
            hz[side, j] = jnp.broadcast_to(zc[j, row : row + 1, :], (64, 128))

    @pl.when(has_south)
    def _():
        for c in south:
            c.wait_send()
        for c in north[:2]:
            c.wait_recv()

    @pl.when(has_north)
    def _():
        for c in north:
            c.wait_send()
        for c in south[:2]:
            c.wait_recv()

    @pl.when(jnp.logical_not(has_north))
    def _():
        clamp(0)

    @pl.when(jnp.logical_not(has_south))
    def _():
        clamp(1)

    for b in range(CHUNKS):

        @pl.when(has_south)
        def _(b=b):
            north[2 + b].wait_recv()

        @pl.when(has_north)
        def _(b=b):
            south[2 + b].wait_recv()

        rim(b * CHUNK, hz, pt, qt, en, gs, put)


def rim(t0, hz, pt, qt, en, gs, put):
    for side in range(2):
        for h in range(8):
            near = 7 - h if side == 0 else h
            lags = tuple(s for s in LAGS if pad_of(s) > 8 * near)
            z = [hz[side, t0 + j, 8 * h : 8 * h + 8, :] for j in range(CHUNK + 2)]
            d = differences(z, lags)
            for k, s in enumerate(LAGS):
                if s not in lags:
                    continue
                if s < 8:
                    at = 0 if side == 0 else 8
                else:
                    at = 8 * h - (64 - s) if side == 0 else 8 * h
                for j in range(CHUNK):
                    pt[k][side, j, at : at + 8, :] = d[s][0][j]
                    qt[k][side, j, at : at + 8, :] = d[s][1][j]
        for g in range(8):
            for j in range(CHUNK):
                to_east = en[side, 0, t0 + j, 8 * g : 8 * g + 8, :]
                to_north = en[side, 1, t0 + j, 8 * g : 8 * g + 8, :]
                for k, s in enumerate(LAGS):
                    if side == 0:
                        if s < 8 and g == 0:
                            at = 8 - s
                        elif s >= 8 and 8 * g < s:
                            at = 8 * g
                        else:
                            continue
                        to_east = to_east + pt[k][0, j, at : at + 8, :]
                        to_north = to_north + qt[k][0, j, at : at + 8, :]
                    else:
                        if s < 8 and g == 7:
                            at = s
                        elif s >= 8 and 8 * g + s >= 64:
                            at = 8 * g + s - 64
                        else:
                            continue
                        to_east = to_east + pt[k][1, j, at : at + 8, :]
                        to_north = to_north - qt[k][1, j, at : at + 8, :]
                row = 8 * g + 192 * side
                columns = pl.ds(128 * (t0 + j), 128)
                put(pl.ds(row, 8), columns, shade(to_east, to_north, gs[row : row + 8, :]))


def store_kernel(i_s, i_f, i_h, o_s, o_f, o_h, sem):
    copies = []
    for k in range(4):
        rows = pl.ds(64 * k, 64)
        copies += [
            pltpu.make_async_copy(i_s.at[rows], o_s.at[rows], sem.at[0, k]),
            pltpu.make_async_copy(i_f.at[0, rows], o_f.at[0, rows], sem.at[1, k]),
            pltpu.make_async_copy(i_f.at[1, rows], o_f.at[1, rows], sem.at[2, k]),
            pltpu.make_async_copy(i_h.at[rows], o_h.at[rows], sem.at[3, k]),
        ]
    for c in copies:
        c.start()
    for c in copies:
        c.wait()


OUTPUTS = ((ROWS, COLS), (2, ROWS, COLS), (ROWS, COLS))


def local(x):
    n_lat, n_lon = lax.axis_size("lat"), lax.axis_size("lon")
    position = lax.axis_index("lat") * ROWS + lax.iota(jnp.int32, ROWS)
    total_rows, total_cols = ROWS * n_lat, COLS * n_lon
    spacing = jnp.sin((position.astype(F32) + 0.5) * (math.pi / total_rows)) * (2.0 * total_rows / total_cols)
    gs = jnp.broadcast_to((1.0 / (56.0 * spacing))[:, None], (ROWS, 128))

    anywhere = pl.BlockSpec(memory_space=pl.ANY)
    vmem = pl.BlockSpec(memory_space=pltpu.VMEM)
    columns = [pltpu.VMEM((TILES, ROWS + 2 * pad_of(s), 128), F32) for s in LAGS]
    near = [pltpu.VMEM((2, CHUNK, pad_of(s) if s >= 8 else 16, 128), F32) for s in LAGS]
    results = pl.pallas_call(
        exchange_kernel,
        out_shape=[pltpu.VMEM(shape, F32) for shape in OUTPUTS],
        in_specs=[pl.BlockSpec(memory_space=pltpu.HBM)] * 2,
        out_specs=[vmem] * 3,
        scratch_shapes=[
            pltpu.VMEM((ROWS, 128), F32),
            pltpu.VMEM((TILES + 2, ROWS, 128), F32),
            pltpu.VMEM((2, TILES + 2, HALO, 128), F32),
            pltpu.VMEM((2, 128, 128), F32),
            pltpu.VMEM((2, 128, 128), F32),
            columns,
            columns,
            pltpu.VMEM((TILES, ROWS, 128), F32),
            pltpu.VMEM((2, 2, TILES, HALO, 128), F32),
            near,
            near,
            pltpu.SemaphoreType.DMA((4, TILES)),
            pltpu.SemaphoreType.DMA((14,)),
            pltpu.SemaphoreType.DMA((14,)),
            pltpu.SemaphoreType.DMA,
        ],
        compiler_params=pltpu.CompilerParams(collective_id=0, has_side_effects=True, vmem_limit_bytes=46 << 20),
        name="exchange",
    )(x, gs)
    return tuple(
        pl.pallas_call(
            store_kernel,
            out_shape=[jax.ShapeDtypeStruct(shape, F32) for shape in OUTPUTS],
            in_specs=[vmem] * 3,
            out_specs=[anywhere] * 3,
            scratch_shapes=[pltpu.SemaphoreType.DMA((4, 4))],
            compiler_params=pltpu.CompilerParams(vmem_limit_bytes=16 << 20),
            name="store",
        )(*results)
    )


def solution(mesh):
    in_specs = (P("lat", "lon"),)
    out_specs = (P("lat", "lon"), P(None, "lat", "lon"), P("lat", "lon"))
    return jax.shard_map(local, mesh=mesh, in_specs=in_specs, out_specs=out_specs, check_vma=False)
```

profile of v0, /device:TPU:218, one launch (start us, length us, event | category | flops | bytes accessed | tf_op | source)
XLA Modules:
  0.0 38.7 jit_solution(17096573408883629004)
XLA Ops:
  0.7 0.8 %broadcast_in_dim.2.scales = f32[256,128]{1,0:T(8,128)} broadcast(f32[256]{0:T(256)S(1)} %multiply_divide_fusion), dimensions={0} | broadcast | bytes 132096 | tf_op jit(solution)/shard_map/broadcast_in_dim | solution.py:337
  1.4 33.8 %exchange.1 = (f32[256,2048]{1,0:T(8,128)S(1)}, f32[2,256,2048]{2,1,0:T(8,128)S(1)}, f32[256,2048]{1,0:T(8,128)S(1)}) custom-call(f32[256,2048]{1,0:T(8,128)} %x.1, f32[256,128]{1,0:T(8,128)} %broadcast_in_dim.2.scales), custom_call_target="tpu_custom_call" | custom-call | tf_op jit(solution)/shard_map/exchange/pallas_call | solution.py:343
  35.3 3.4 %store.1 = (f32[256,2048]{1,0:T(8,128)}, f32[2,256,2048]{2,1,0:T(8,128)}, f32[256,2048]{1,0:T(8,128)}) custom-call(f32[256,2048]{1,0:T(8,128)S(1)} %get-tuple-element.6.i_s, f32[2,256,2048]{2,1,0:T(8,128)S(1)} %get-tuple-element.7.i_f, f32[256,2048]{1,0:T(8,128)S(1)} %get-tuple-element.8.i_h), custom_call_target="tpu_custom_call" | custom-call | tf_op jit(solution)/shard_map/store/pallas_call | solution.py:369
  (1 shorter events, 0.0 us)
where the time goes:
time: 38.8 us; the launch traced here: 38.7 us
  Pallas kernels  37.3 us (96%)
  local copies, waits for them, and re-layouts  0.77 us (2%)
  between operations  0.64 us (2%)
    pallas_call x1, Pallas kernels, local(): pl.pallas_call(exchange_kernel, out_shape=[pltpu.VMEM(shape, F32) for sha...  33.8 us
    pallas_call x1, Pallas kernels, local(): pl.pallas_call(store_kernel, out_shape=[jax.ShapeDtypeStruct(shape, F32)...  3.42 us

commit v1 on v0

--- a/solution.py
+++ b/solution.py
@@ -17,42 +17,61 @@
     return max(8, s)
 
 
+SMALLEST = 1.1754944e-38
+
+
 def shade(east, north, east_scale):
     grad_east = east * east_scale
     grad_north = north * (1.0 / 56.0)
     squared = grad_east * grad_east + grad_north * grad_north
     inverse = lax.rsqrt(1.0 + squared)
-    a = jnp.sqrt(squared) * inverse
+    a = squared * lax.rsqrt(jnp.maximum(squared, SMALLEST)) * inverse
     b = 1.0 + inverse
     upper = a > 0.41421356 * b
     v = jnp.where(upper, a - b, a) / jnp.where(upper, a + b, b)
     z = v * v
-    poly = ((8.05374449538e-2 * z - 1.38776856032e-1) * z + 1.99777106478e-1) * z - 3.33329491539e-1
-    slope = 2.0 * (poly * z * v + v + jnp.where(upper, math.pi / 4, 0.0))
-    facing_east = -grad_east * inverse
-    facing_north = -grad_north * inverse
-    shading = jnp.maximum(0.5 * (facing_north - facing_east) + math.sqrt(0.5) * inverse, 0.0)
+    poly = ((2 * 8.05374449538e-2 * z - 2 * 1.38776856032e-1) * z + 2 * 1.99777106478e-1) * z - 2 * 3.33329491539e-1
+    slope = (poly * z + 2.0) * v + jnp.where(upper, math.pi / 2, 0.0)
+    down = -inverse
+    facing_east = grad_east * down
+    facing_north = grad_north * down
+    shading = jnp.maximum((0.5 * (grad_east - grad_north) + math.sqrt(0.5)) * inverse, 0.0)
     return slope, facing_east, facing_north, shading
 
 
-def differences(z, lags):
+def differences(tiles, count, lags):
     lane = lax.broadcasted_iota(jnp.int32, (8, 128), 1)
-    out = {}
-    for s in lags:
-        right = [pltpu.roll(t, s, 1) for t in z[:-1]]
+    scaled, right, left = {}, {}, {}
+
+    def at(j, s):
+        if (j, s) not in scaled:
+            if s == 0.5:
+                scaled[j, s] = 2.0 * at(j, 1)
+            elif s == 1:
+                scaled[j, s] = tiles(j)
+            else:
+                scaled[j, s] = at(j, 1) * (1.0 / s)
+        return scaled[j, s]
+
+    def turned(j, s):
+        if (j, s) not in right:
+            right[j, s] = pltpu.roll(at(j, s), s, 1)
+        return right[j, s]
+
+    def turned_back(j, s):
         if s == 64:
-            left = [pltpu.roll(z[-1], 64, 1)]
-            left = right[1:] + left
-        else:
-            left = [pltpu.roll(t, 128 - s, 1) for t in z[1:]]
-        p, q = [], []
-        for j in range(len(z) - 2):
-            west = jnp.where(lane < s, right[j], right[j + 1])
-            east = jnp.where(lane < 128 - s, left[j], left[j + 1])
-            p.append((east - west) * (1.0 / s))
-            q.append((east + west + 2.0 * z[j + 1]) * (1.0 / s))
-        out[s] = (p, q)
-    return out
+            return turned(j, s)
+        if (j, s) not in left:
+            left[j, s] = pltpu.roll(at(j, s), 128 - s, 1)
+        return left[j, s]
+
+    for j in range(count):
+        out = {}
+        for s in lags:
+            west = jnp.where(lane < s, turned(j, s), turned(j + 1, s))
+            east = jnp.where(lane < 128 - s, turned_back(j + 1, s), turned_back(j + 2, s))
+            out[s] = (east - west, east + west + at(j + 1, s / 2 if s > 1 else 0.5))
+        yield j, out
 
 
 CHUNK = 4
@@ -61,7 +80,7 @@
 
 
 def exchange_kernel(
-    x, scales, o_s, o_f, o_h, gs, zc, hz, packed, arrived, ps, qs, cs, en, pt, qt, sem_in, sem_out, sem_got, sem_gs
+    x, o_s, o_f, o_h, gs, zc, hz, packed, arrived, ps, qs, cs, en, pt, qt, sem_in, sem_out, sem_got
 ):
     lat, lon = lax.axis_index("lat"), lax.axis_index("lon")
     n_lat, n_lon = lax.axis_size("lat"), lax.axis_size("lon")
@@ -78,8 +97,6 @@
     middle = [load(k, j) for k in (1, 2) for j in range(1, TILES - 1)]
     for c in edges + rims + middle:
         c.start()
-    scale_copy = pltpu.make_async_copy(scales, gs, sem_gs)
-    scale_copy.start()
 
     barrier = pltpu.get_barrier_semaphore()
 
@@ -101,6 +118,20 @@
         for to in (lon, east, west):
             greet(lat + 1, to)
 
+    total_rows, total_cols = ROWS * n_lat, COLS * n_lon
+    position = (lat * ROWS + lax.broadcasted_iota(jnp.int32, (ROWS, 128), 0)).astype(F32)
+    spacing = jnp.sin((position + 0.5) * (math.pi / total_rows)) * (2.0 * total_rows / total_cols)
+    gs[...] = 1.0 / (56.0 * spacing)
+    for k, s in enumerate(LAGS):
+        m = pad_of(s)
+        for ref in (ps[k], qs[k]):
+            ref[:, 0:m, :] = jnp.zeros((TILES, m, 128), F32)
+            ref[:, m + ROWS : m + ROWS + m, :] = jnp.zeros((TILES, m, 128), F32)
+    zero = jnp.zeros((CHUNK, 8, 128), F32)
+    for k in range(3):
+        for ref in (pt[k], qt[k]):
+            ref[0, :, 8:16, :] = zero
+            ref[1, :, 0:8, :] = zero
     lane = lax.broadcasted_iota(jnp.int32, (128, 128), 1)
     for c in edges:
         c.wait()
@@ -149,35 +180,18 @@
         for c in north:
             c.start()
 
-    for k, s in enumerate(LAGS):
-        m = pad_of(s)
-        for ref in (ps[k], qs[k]):
-            ref[:, 0:m, :] = jnp.zeros((TILES, m, 128), F32)
-            ref[:, m + ROWS : m + ROWS + m, :] = jnp.zeros((TILES, m, 128), F32)
-    zero = jnp.zeros((CHUNK, 8, 128), F32)
-    for k in range(3):
-        for ref in (pt[k], qt[k]):
-            ref[0, :, 8:16, :] = zero
-            ref[1, :, 0:8, :] = zero
     for c in middle:
         c.wait()
-    scale_copy.wait()
-    for c in along:
-        c.wait()
-    zc[0, 0:128, :] = pltpu.roll(arrived[0], 64, 1)
-    zc[0, 128:256, :] = arrived[0]
-    zc[17, 0:128, :] = arrived[1]
-    zc[17, 128:256, :] = pltpu.roll(arrived[1], 64, 1)
-
-    def first(row):
-        z = [zc[j, pl.ds(row, 8), :] for j in range(TILES + 2)]
-        d = differences(z, LAGS)
-        for k, s in enumerate(LAGS):
-            for j in range(TILES):
-                ps[k][j, pl.ds(row + pad_of(s), 8), :] = d[s][0][j]
-                qs[k][j, pl.ds(row + pad_of(s), 8), :] = d[s][1][j]
-        for j in range(TILES):
-            cs[j, pl.ds(row, 8), :] = 2.0 * sum(d[s][0][j] for s in LAGS)
+
+    def first(row, t0=0, count=TILES):
+        for i, d in differences(lambda j: zc[t0 + j, pl.ds(row, 8), :], count, LAGS):
+            j = t0 + i
+            total = None
+            for k, s in enumerate(LAGS):
+                ps[k][j, pl.ds(row + pad_of(s), 8), :] = d[s][0]
+                qs[k][j, pl.ds(row + pad_of(s), 8), :] = d[s][1]
+                total = d[s][0] if total is None else total + d[s][0]
+            cs[j, pl.ds(row, 8), :] = 2.0 * total
 
     def second(row, j):
         to_east = cs[j, pl.ds(row, 8), :]
@@ -190,18 +204,23 @@
             to_north = diff if to_north is None else to_north + diff
         return to_east, to_north
 
-    def partial(row, side, to):
-        for j in range(TILES):
-            to_east, to_north = second(row, j)
-            en[side, 0, j, pl.ds(to, 8), :] = to_east
-            en[side, 1, j, pl.ds(to, 8), :] = to_north
-
     def put(rows, columns, values):
         o_s[rows, columns] = values[0]
         o_f[0, rows, columns] = values[1]
         o_f[1, rows, columns] = values[2]
         o_h[rows, columns] = values[3]
 
+    def partial(row, side, to, tiles):
+        for j in tiles:
+            to_east, to_north = second(row, j)
+            en[side, 0, j, pl.ds(to, 8), :] = to_east
+            en[side, 1, j, pl.ds(to, 8), :] = to_north
+
+    def finish(row, tiles):
+        scale = gs[pl.ds(row, 8), :]
+        for j in tiles:
+            put(pl.ds(row, 8), pl.ds(128 * j, 128), shade(*second(row, j), scale))
+
     def loop(lo, hi, body):
         def step(i, carry):
             body(pl.multiple_of(8 * i, 8))
@@ -209,21 +228,49 @@
 
         lax.fori_loop(lo, hi, step, 0)
 
+    def back(row, by):
+        return pl.multiple_of(row - by, 8)
+
+    inner = range(1, TILES - 1)
+
     def with_top(row):
-        first(row)
-        partial(pl.multiple_of(row - 64, 8), 0, pl.multiple_of(row - 64, 8))
+        first(row, 1, TILES - 2)
+        partial(back(row, 64), 0, back(row, 64), inner)
 
     def with_middle(row):
-        first(row)
-        here = pl.multiple_of(row - 64, 8)
-        scale = gs[pl.ds(here, 8), :]
-        for j in range(TILES):
-            put(pl.ds(here, 8), pl.ds(128 * j, 128), shade(*second(here, j), scale))
-
-    loop(0, 8, first)
+        first(row, 1, TILES - 2)
+        finish(back(row, 64), inner)
+
+    loop(0, 8, lambda row: first(row, 1, TILES - 2))
     loop(8, 16, with_top)
     loop(16, 32, with_middle)
-    loop(24, 32, lambda row: partial(row, 1, pl.multiple_of(row - 192, 8)))
+    loop(24, 32, lambda row: partial(row, 1, back(row, 192), inner))
+
+    for c in along:
+        c.wait()
+    zc[0, 0:128, :] = pltpu.roll(arrived[0], 64, 1)
+    zc[0, 128:256, :] = arrived[0]
+    zc[17, 0:128, :] = arrived[1]
+    zc[17, 128:256, :] = pltpu.roll(arrived[1], 64, 1)
+
+    outer = (0, TILES - 1)
+
+    def ends(row):
+        for r in range(4):
+            for j in outer:
+                first(row * 4 + 8 * r, j, 1)
+
+    def ends_rims(row):
+        partial(row, 0, row, outer)
+        partial(row + 192, 1, row, outer)
+
+    def ends_middle(row):
+        for r in range(4):
+            finish(64 + row * 4 + 8 * r, outer)
+
+    loop(0, 8, ends)
+    loop(0, 8, ends_rims)
+    loop(0, 4, ends_middle)
 
     def clamp(side):
         row = 0 if side == 0 else ROWS - 1
@@ -270,18 +317,14 @@
         for h in range(8):
             near = 7 - h if side == 0 else h
             lags = tuple(s for s in LAGS if pad_of(s) > 8 * near)
-            z = [hz[side, t0 + j, 8 * h : 8 * h + 8, :] for j in range(CHUNK + 2)]
-            d = differences(z, lags)
-            for k, s in enumerate(LAGS):
-                if s not in lags:
-                    continue
-                if s < 8:
-                    at = 0 if side == 0 else 8
-                else:
-                    at = 8 * h - (64 - s) if side == 0 else 8 * h
-                for j in range(CHUNK):
-                    pt[k][side, j, at : at + 8, :] = d[s][0][j]
-                    qt[k][side, j, at : at + 8, :] = d[s][1][j]
+            for j, d in differences(lambda j: hz[side, t0 + j, 8 * h : 8 * h + 8, :], CHUNK, lags):
+                for s in lags:
+                    if s < 8:
+                        at = 0 if side == 0 else 8
+                    else:
+                        at = 8 * h - (64 - s) if side == 0 else 8 * h
+                    pt[LAGS.index(s)][side, j, at : at + 8, :] = d[s][0]
+                    qt[LAGS.index(s)][side, j, at : at + 8, :] = d[s][1]
         for g in range(8):
             for j in range(CHUNK):
                 to_east = en[side, 0, t0 + j, 8 * g : 8 * g + 8, :]
@@ -330,12 +373,6 @@
 
 
 def local(x):
-    n_lat, n_lon = lax.axis_size("lat"), lax.axis_size("lon")
-    position = lax.axis_index("lat") * ROWS + lax.iota(jnp.int32, ROWS)
-    total_rows, total_cols = ROWS * n_lat, COLS * n_lon
-    spacing = jnp.sin((position.astype(F32) + 0.5) * (math.pi / total_rows)) * (2.0 * total_rows / total_cols)
-    gs = jnp.broadcast_to((1.0 / (56.0 * spacing))[:, None], (ROWS, 128))
-
     anywhere = pl.BlockSpec(memory_space=pl.ANY)
     vmem = pl.BlockSpec(memory_space=pltpu.VMEM)
     columns = [pltpu.VMEM((TILES, ROWS + 2 * pad_of(s), 128), F32) for s in LAGS]
@@ -343,7 +380,7 @@
     results = pl.pallas_call(
         exchange_kernel,
         out_shape=[pltpu.VMEM(shape, F32) for shape in OUTPUTS],
-        in_specs=[pl.BlockSpec(memory_space=pltpu.HBM)] * 2,
+        in_specs=[pl.BlockSpec(memory_space=pltpu.HBM)],
         out_specs=[vmem] * 3,
         scratch_shapes=[
             pltpu.VMEM((ROWS, 128), F32),
@@ -360,11 +397,10 @@
             pltpu.SemaphoreType.DMA((4, TILES)),
             pltpu.SemaphoreType.DMA((14,)),
             pltpu.SemaphoreType.DMA((14,)),
-            pltpu.SemaphoreType.DMA,
         ],
         compiler_params=pltpu.CompilerParams(collective_id=0, has_side_effects=True, vmem_limit_bytes=46 << 20),
         name="exchange",
-    )(x, gs)
+    )(x)
     return tuple(
         pl.pallas_call(
             store_kernel,

time: 38.8 us -> 30.1 us (0.78)
  the two profiles are of different devices: /device:TPU:218 before, /device:TPU:192 now
where the time goes in v1:
time: 30.1 us; the launch traced here: 29.9 us
  Pallas kernels  29.3 us (97%)
  between operations  0.64 us (2%)
    pallas_call x1, Pallas kernels, local(): pl.pallas_call(exchange_kernel, out_shape=[pltpu.VMEM(shape, F32) for sha...  25.9 us
    pallas_call x1, Pallas kernels, local(): pl.pallas_call(store_kernel, out_shape=[jax.ShapeDtypeStruct(shape, F32)...  3.42 us

profile of v1, /device:TPU:192, one launch (start us, length us, event | category | flops | bytes accessed | tf_op | source)
XLA Modules:
  0.0 29.9 jit_solution(7021706192514187029)
XLA Ops:
  0.6 25.9 %exchange.1 = (f32[256,2048]{1,0:T(8,128)S(1)}, f32[2,256,2048]{2,1,0:T(8,128)S(1)}, f32[256,2048]{1,0:T(8,128)S(1)}) custom-call(f32[256,2048]{1,0:T(8,128)} %x.1), custom_call_target="tpu_custom_call" | custom-call | tf_op jit(solution)/shard_map/exchange/pallas_call | solution.py:380
  26.5 3.4 %store.1 = (f32[256,2048]{1,0:T(8,128)}, f32[2,256,2048]{2,1,0:T(8,128)}, f32[256,2048]{1,0:T(8,128)}) custom-call(f32[256,2048]{1,0:T(8,128)S(1)} %get-tuple-element.6.i_s, f32[2,256,2048]{2,1,0:T(8,128)S(1)} %get-tuple-element.7.i_f, f32[256,2048]{1,0:T(8,128)S(1)} %get-tuple-element.8.i_h), custom_call_target="tpu_custom_call" | custom-call | tf_op jit(solution)/shard_map/store/pallas_call | solution.py:405

commit v2 on v1

v2 whole, which is shorter than its diff:
```python
import math

import jax
import jax.numpy as jnp
from jax import lax
from jax.experimental import pallas as pl
from jax.experimental.pallas import tpu as pltpu
from jax.sharding import PartitionSpec as P

HALO = 64
LAGS = (1, 2, 4, 8, 16, 32, 64)
F32 = jnp.float32
ROWS, COLS, TILES = 256, 2048, 16


def pad_of(s):
    return max(8, s)


SMALLEST = 1.1754944e-38


def shade(east, north, east_scale):
    grad_east = east * east_scale
    grad_north = north * (1.0 / 56.0)
    squared = grad_east * grad_east + grad_north * grad_north
    inverse = lax.rsqrt(1.0 + squared)
    a = squared * lax.rsqrt(jnp.maximum(squared, SMALLEST)) * inverse
    b = 1.0 + inverse
    upper = a > 0.41421356 * b
    v = jnp.where(upper, a - b, a) / jnp.where(upper, a + b, b)
    z = v * v
    poly = ((2 * 8.05374449538e-2 * z - 2 * 1.38776856032e-1) * z + 2 * 1.99777106478e-1) * z - 2 * 3.33329491539e-1
    slope = (poly * z + 2.0) * v + jnp.where(upper, math.pi / 2, 0.0)
    down = -inverse
    facing_east = grad_east * down
    facing_north = grad_north * down
    shading = jnp.maximum((0.5 * (grad_east - grad_north) + math.sqrt(0.5)) * inverse, 0.0)
    return slope, facing_east, facing_north, shading


def differences(tiles, count, lags):
    lane = lax.broadcasted_iota(jnp.int32, (8, 128), 1)
    scaled, right, left = {}, {}, {}

    def at(j, s):
        if (j, s) not in scaled:
            if s == 0.5:
                scaled[j, s] = 2.0 * at(j, 1)
            elif s == 1:
                scaled[j, s] = tiles(j)
            else:
                scaled[j, s] = at(j, 1) * (1.0 / s)
        return scaled[j, s]

    def turned(j, s):
        if (j, s) not in right:
            right[j, s] = pltpu.roll(at(j, s), s, 1)
        return right[j, s]

    def turned_back(j, s):
        if s == 64:
            return turned(j, s)
        if (j, s) not in left:
            left[j, s] = pltpu.roll(at(j, s), 128 - s, 1)
        return left[j, s]

    for j in range(count):
        out = {}
        for s in lags:
            west = jnp.where(lane < s, turned(j, s), turned(j + 1, s))
            east = jnp.where(lane < 128 - s, turned_back(j + 1, s), turned_back(j + 2, s))
            out[s] = (east - west, east + west + at(j + 1, s / 2 if s > 1 else 0.5))
        yield j, out


BLOCKS = ((1, 4), (5, 4), (9, 4), (13, 2))
SPANS = ((0, 6), (6, 4), (10, 4), (14, 2))
MOST = 4
ENDS = (0, TILES - 1)


def clear(pt, qt):
    for k in range(3):
        for ref in (pt[k], qt[k]):
            zero = jnp.zeros((ref.shape[1], 8, 128), F32)
            ref[0, :, 8:16, :] = zero
            ref[1, :, 0:8, :] = zero


def halo_differences(side, tiles, at, count, pt, qt):
    for h in range(8):
        near = 7 - h if side == 0 else h
        lags = tuple(s for s in LAGS if pad_of(s) > 8 * near)
        for j, d in differences(lambda j, h=h: tiles(h, j), count, lags):
            for s in lags:
                if s < 8:
                    row = 0 if side == 0 else 8
                else:
                    row = 8 * h - (64 - s) if side == 0 else 8 * h
                k = LAGS.index(s)
                pt[k][side, at + j, row : row + 8, :] = d[s][0]
                qt[k][side, at + j, row : row + 8, :] = d[s][1]


def halo_sums(side, g, j, pt, qt, to_east, to_north):
    for k, s in enumerate(LAGS):
        if side == 0:
            if s < 8 and g == 0:
                row = 8 - s
            elif s >= 8 and 8 * g < s:
                row = 8 * g
            else:
                continue
            to_north = to_north + qt[k][0, j, row : row + 8, :]
        else:
            if s < 8 and g == 7:
                row = s
            elif s >= 8 and 8 * g + s >= 64:
                row = 8 * g + s - 64
            else:
                continue
            to_north = to_north - qt[k][1, j, row : row + 8, :]
        to_east = to_east + pt[k][side, j, row : row + 8, :]
    return to_east, to_north


def loop(lo, hi, body):
    def step(i, carry):
        body(pl.multiple_of(8 * i, 8))
        return carry

    lax.fori_loop(lo, hi, step, 0)


def exchange_kernel(
    x, o_s, o_f, o_h, hz, ends, gs, arrived, corners, zc, packed, ps, qs, cs, en, pt, qt, sem_in, sem_out, sem_got
):
    lat, lon = lax.axis_index("lat"), lax.axis_index("lon")
    n_lat, n_lon = lax.axis_size("lat"), lax.axis_size("lon")
    east, west = lax.rem(lon + 1, n_lon), lax.rem(lon + n_lon - 1, n_lon)
    has_north, has_south = lat > 0, lat < n_lat - 1

    def load(k, j):
        return pltpu.make_async_copy(
            x.at[pl.ds(64 * k, 64), pl.ds(128 * j, 128)], zc.at[j + 1, pl.ds(64 * k, 64)], sem_in.at[k, j]
        )

    rims = [load(k, j) for k in (0, 3) for j in range(TILES)]
    middle = [load(k, j) for k in (1, 2) for j in range(TILES)]
    for c in rims + middle:
        c.start()

    barrier = pltpu.get_barrier_semaphore()

    def greet(to_lat, to_lon):
        pl.semaphore_signal(
            barrier, inc=1, device_id={"lat": to_lat, "lon": to_lon}, device_id_type=pl.DeviceIdType.MESH
        )

    greet(lat, east)
    greet(lat, west)

    @pl.when(has_north)
    def _():
        for to in (lon, east, west):
            greet(lat - 1, to)

    @pl.when(has_south)
    def _():
        for to in (lon, east, west):
            greet(lat + 1, to)

    total_rows, total_cols = ROWS * n_lat, COLS * n_lon
    position = (lat * ROWS + lax.broadcasted_iota(jnp.int32, (ROWS, 128), 0)).astype(F32)
    spacing = jnp.sin((position + 0.5) * (math.pi / total_rows)) * (2.0 * total_rows / total_cols)
    gs[...] = 1.0 / (56.0 * spacing)
    for c in rims:
        c.wait()

    def send(src, dst, k, to_lat, to_lon):
        return pltpu.make_async_remote_copy(
            src_ref=src,
            dst_ref=dst,
            send_sem=sem_out.at[k],
            recv_sem=sem_got.at[k],
            device_id={"lat": to_lat, "lon": to_lon},
            device_id_type=pl.DeviceIdType.MESH,
        )

    south, north = [], []
    for k, (at, n) in enumerate(SPANS):
        tiles = pl.ds(1 + at, n)
        south.append(send(zc.at[tiles, pl.ds(192, 64)], hz.at[0, tiles], 6 + k, lat + 1, lon))
        north.append(send(zc.at[tiles, pl.ds(0, 64)], hz.at[1, tiles], 10 + k, lat - 1, lon))
    along = [send(packed.at[0], arrived.at[0], 0, lat, east), send(packed.at[1], arrived.at[1], 1, lat, west)]
    top, bottom = pl.ds(0, 32), pl.ds(96, 32)
    south_corners = [
        send(packed.at[0, bottom], corners.at[0, 0], 2, lat + 1, east),
        send(packed.at[1, bottom], corners.at[0, 1], 3, lat + 1, west),
    ]
    north_corners = [
        send(packed.at[0, top], corners.at[1, 0], 4, lat - 1, east),
        send(packed.at[1, top], corners.at[1, 1], 5, lat - 1, west),
    ]

    inside = jnp.logical_and(has_north, has_south)
    pl.semaphore_wait(barrier, jnp.where(inside, 8, 5))
    for k in range(len(SPANS)):
        for c, there in ((south[k], has_south), (north[k], has_north)):

            @pl.when(there)
            def _(c=c):
                c.start()

    for c in middle:
        c.wait()
    low = lax.broadcasted_iota(jnp.int32, (32, 128), 1) < 64
    for k in range(4):
        one, two, to = slice(64 * k, 64 * k + 32), slice(64 * k + 32, 64 * k + 64), slice(32 * k, 32 * k + 32)
        packed[0, to, :] = jnp.where(low, pltpu.roll(zc[TILES, one, :], 64, 1), zc[TILES, two, :])
        packed[1, to, :] = jnp.where(low, zc[1, one, :], pltpu.roll(zc[1, two, :], 64, 1))

    for j in (0, TILES + 1):
        zc[j] = jnp.zeros((ROWS, 128), F32)
    for k, s in enumerate(LAGS):
        m = pad_of(s)
        for ref in (ps[k], qs[k]):
            ref[:, 0:m, :] = jnp.zeros((TILES, m, 128), F32)
            ref[:, m + ROWS : m + ROWS + m, :] = jnp.zeros((TILES, m, 128), F32)
    clear(pt, qt)

    for c in along:
        c.start()

    @pl.when(has_south)
    def _():
        for c in south_corners:
            c.start()

    @pl.when(has_north)
    def _():
        for c in north_corners:
            c.start()

    def first(row):
        for j, d in differences(lambda j: zc[j, pl.ds(row, 8), :], TILES, LAGS):
            total = None
            for k, s in enumerate(LAGS):
                ps[k][j, pl.ds(row + pad_of(s), 8), :] = d[s][0]
                qs[k][j, pl.ds(row + pad_of(s), 8), :] = d[s][1]
                total = d[s][0] if total is None else total + d[s][0]
            cs[j, pl.ds(row, 8), :] = 2.0 * total

    def second(row, j):
        to_east = cs[j, pl.ds(row, 8), :]
        to_north = None
        for k, s in enumerate(LAGS):
            m = pad_of(s)
            above, below = pl.ds(row + (m - s), 8), pl.ds(row + (m + s), 8)
            to_east = to_east + (ps[k][j, above, :] + ps[k][j, below, :])
            diff = qs[k][j, above, :] - qs[k][j, below, :]
            to_north = diff if to_north is None else to_north + diff
        return to_east, to_north

    def put(rows, j, values):
        columns = slice(128 * j, 128 * j + 128)
        o_s[rows, columns] = values[0]
        o_f[0, rows, columns] = values[1]
        o_f[1, rows, columns] = values[2]
        o_h[rows, columns] = values[3]

    def keep_ends(row):
        for k, j in enumerate(ENDS):
            ends[k, 0, pl.ds(row, 8), :], ends[k, 1, pl.ds(row, 8), :] = second(row, j)

    def partial(row, side, to):
        for j in range(1, TILES - 1):
            en[side, 0, j, pl.ds(to, 8), :], en[side, 1, j, pl.ds(to, 8), :] = second(row, j)
        keep_ends(row)

    def finish(row):
        scale = gs[pl.ds(row, 8), :]
        for j in range(1, TILES - 1):
            put(pl.ds(row, 8), j, shade(*second(row, j), scale))
        keep_ends(row)

    def back(row, by):
        return pl.multiple_of(row - by, 8)

    def with_top(row):
        first(row)
        partial(back(row, 64), 0, back(row, 64))

    def with_middle(row):
        first(row)
        finish(back(row, 64))

    loop(0, 8, first)
    loop(8, 16, with_top)
    loop(16, 32, with_middle)
    loop(24, 32, lambda row: partial(row, 1, back(row, 192)))

    def clamp(side):
        row = 0 if side == 0 else ROWS - 1
        for j in range(1, TILES + 1):
            hz[side, j] = jnp.broadcast_to(zc[j, row : row + 1, :], (64, 128))

    @pl.when(jnp.logical_not(has_north))
    def _():
        clamp(0)

    @pl.when(jnp.logical_not(has_south))
    def _():
        clamp(1)

    for b, (at, n) in enumerate(BLOCKS):

        @pl.when(has_south)
        def _(b=b):
            north[b].wait_recv()

        @pl.when(has_north)
        def _(b=b):
            south[b].wait_recv()

        for side in range(2):
            halo_differences(
                side, lambda h, j, side=side, at=at: hz[side, at + j, 8 * h : 8 * h + 8, :], 0, n, pt, qt
            )
            for g in range(8):
                for j in range(n):
                    rows = slice(8 * g, 8 * g + 8)
                    sums = halo_sums(side, g, j, pt, qt, en[side, 0, at + j, rows, :], en[side, 1, at + j, rows, :])
                    rows = slice(8 * g + 192 * side, 8 * g + 192 * side + 8)
                    put(rows, at + j, shade(*sums, gs[rows, :]))

    for c in along:
        c.wait()

    @pl.when(has_south)
    def _():
        for c in north_corners:
            c.wait_recv()
        for c in south + south_corners:
            c.wait_send()

    @pl.when(has_north)
    def _():
        for c in south_corners:
            c.wait_recv()
        for c in north + north_corners:
            c.wait_send()


def store_kernel(
    i_s, i_f, i_h, hz, ends, gs, arrived, corners, o_s, o_f, o_h, hc, outer, pt, qt, stage, sem, sem_ends
):
    lat, n_lat = lax.axis_index("lat"), lax.axis_size("lat")

    def pieces(at):
        return (
            (i_s.at[at], o_s.at[at]),
            (i_f.at[(0, *at)], o_f.at[(0, *at)]),
            (i_f.at[(1, *at)], o_f.at[(1, *at)]),
            (i_h.at[at], o_h.at[at]),
        )

    copies = []
    for k in range(4):
        for n, (src, dst) in enumerate(pieces((pl.ds(64 * k, 64), pl.ds(128, COLS - 256)))):
            copies.append(pltpu.make_async_copy(src, dst, sem.at[n, k]))
    for c in copies:
        c.start()

    clear(pt, qt)
    for k, s in enumerate(LAGS):
        m = pad_of(s)
        outer[k][:, 0:m, :] = jnp.zeros((2, m, 128), F32)
        outer[k][:, m + ROWS : m + ROWS + m, :] = jnp.zeros((2, m, 128), F32)

    for side in range(2):
        pole = lat == (0 if side == 0 else n_lat - 1)

        @pl.when(jnp.logical_not(pole))
        def _(side=side):
            for e in range(2):
                both = corners[side, e]
                turned = pltpu.roll(both, 64, 1)
                hc[side, e, 0:32, :] = turned if e == 0 else both
                hc[side, e, 32:64, :] = both if e == 0 else turned

        @pl.when(pole)
        def _(side=side):
            for e in range(2):
                both = arrived[e, 0:8, :] if side == 0 else arrived[e, 120:128, :]
                turned = pltpu.roll(both, 64, 1)
                block = turned if (e == 0) == (side == 0) else both
                line = block[0:1] if side == 0 else block[7:8]
                hc[side, e] = jnp.broadcast_to(line, (64, 128))

    lane = lax.broadcasted_iota(jnp.int32, (8, 128), 1)

    def beyond(row):
        for r in range(8):
            half = 0 if r < 4 else 1
            at = pl.multiple_of(row * 4 + 8 * (r % 4), 8)
            to = pl.multiple_of(row * 8 + 8 * r, 8)
            for e in range(2):
                z = arrived[e, pl.ds(at, 8), :]
                for k, s in enumerate(LAGS):
                    by = (s + (64 if half == 0 else 0)) % 128 if e == 0 else (256 - s - (64 if half else 0)) % 128
                    turned = pltpu.roll(z, by, 1) if by else z
                    inside = lane < s if e == 0 else lane >= 128 - s
                    value = jnp.where(inside, turned * ((-1.0 if e == 0 else 1.0) / s), 0.0)
                    outer[k][e, pl.ds(to + pad_of(s), 8), :] = value

    loop(0, 4, beyond)

    for side in range(2):
        for e in range(2):

            def tiles(h, j, side=side, e=e):
                rows = slice(8 * h, 8 * h + 8)
                if e == 0:
                    return hc[side, 0, rows, :] if j == 0 else hz[side, j, rows, :]
                return hc[side, 1, rows, :] if j == 2 else hz[side, TILES - 1 + j, rows, :]

            halo_differences(side, tiles, e, 1, pt, qt)

    def sums(row, e):
        to_east = ends[e, 0, pl.ds(row, 8), :]
        to_north = ends[e, 1, pl.ds(row, 8), :]
        for k, s in enumerate(LAGS):
            m = pad_of(s)
            here = outer[k][e, pl.ds(row + m, 8), :]
            above = outer[k][e, pl.ds(row + (m - s), 8), :]
            below = outer[k][e, pl.ds(row + (m + s), 8), :]
            to_east = to_east + (above + below + 2.0 * here)
            diff = above - below
            to_north = to_north - diff if e == 0 else to_north + diff
        return to_east, to_north

    def put(row, e, values):
        for n, v in enumerate(values):
            stage[n, e, pl.ds(row, 8), :] = v

    def flush(k):
        for n in range(4):
            for e in range(2):
                at = (pl.ds(64 * k, 64), pl.ds(128 * ENDS[e], 128))
                dst = (o_s.at[at], o_f.at[(0, *at)], o_f.at[(1, *at)], o_h.at[at])[n]
                c = pltpu.make_async_copy(stage.at[n, e, pl.ds(64 * k, 64)], dst, sem_ends.at[n, e, k])
                c.start()
                copies.append(c)

    def middle(row):
        for r in range(4):
            here = pl.multiple_of(64 + row * 4 + 8 * r, 8)
            for e in range(2):
                put(here, e, shade(*sums(here, e), gs[pl.ds(here, 8), :]))

    loop(0, 4, middle)
    flush(1)
    flush(2)
    for side in range(2):
        for g in range(8):
            row = 8 * g + 192 * side
            for e in range(2):
                both = halo_sums(side, g, e, pt, qt, *sums(row, e))
                put(row, e, shade(*both, gs[row : row + 8, :]))
        flush(3 * side)
    for c in copies:
        c.wait()


OUTPUTS = ((ROWS, COLS), (2, ROWS, COLS), (ROWS, COLS))
BETWEEN = (
    (2, TILES + 2, HALO, 128),
    (2, 2, ROWS, 128),
    (ROWS, 128),
    (2, ROWS // 2, 128),
    (2, 2, HALO // 2, 128),
)


def local(x):
    anywhere = pl.BlockSpec(memory_space=pl.ANY)
    vmem = pl.BlockSpec(memory_space=pltpu.VMEM)
    columns = [pltpu.VMEM((TILES, ROWS + 2 * pad_of(s), 128), F32) for s in LAGS]

    def near(count):
        return [pltpu.VMEM((2, count, pad_of(s) if s >= 8 else 16, 128), F32) for s in LAGS]

    results = pl.pallas_call(
        exchange_kernel,
        out_shape=[pltpu.VMEM(shape, F32) for shape in OUTPUTS + BETWEEN],
        in_specs=[pl.BlockSpec(memory_space=pltpu.HBM)],
        out_specs=[vmem] * len(OUTPUTS + BETWEEN),
        scratch_shapes=[
            pltpu.VMEM((TILES + 2, ROWS, 128), F32),
            pltpu.VMEM((2, 128, 128), F32),
            columns,
            columns,
            pltpu.VMEM((TILES, ROWS, 128), F32),
            pltpu.VMEM((2, 2, TILES, HALO, 128), F32),
            near(MOST),
            near(MOST),
            pltpu.SemaphoreType.DMA((4, TILES)),
            pltpu.SemaphoreType.DMA((14,)),
            pltpu.SemaphoreType.DMA((14,)),
        ],
        compiler_params=pltpu.CompilerParams(collective_id=0, has_side_effects=True, vmem_limit_bytes=46 << 20),
        name="exchange",
    )(x)
    return tuple(
        pl.pallas_call(
            store_kernel,
            out_shape=[jax.ShapeDtypeStruct(shape, F32) for shape in OUTPUTS],
            in_specs=[vmem] * len(OUTPUTS + BETWEEN),
            out_specs=[anywhere] * 3,
            scratch_shapes=[
                pltpu.VMEM((2, 2, HALO, 128), F32),
                [pltpu.VMEM((2, ROWS + 2 * pad_of(s), 128), F32) for s in LAGS],
                near(2),
                near(2),
                pltpu.VMEM((4, 2, ROWS, 128), F32),
                pltpu.SemaphoreType.DMA((4, 4)),
                pltpu.SemaphoreType.DMA((4, 2, 4)),
            ],
            compiler_params=pltpu.CompilerParams(vmem_limit_bytes=16 << 20),
            name="store",
        )(*results)
    )


def solution(mesh):
    in_specs = (P("lat", "lon"),)
    out_specs = (P("lat", "lon"), P(None, "lat", "lon"), P("lat", "lon"))
    return jax.shard_map(local, mesh=mesh, in_specs=in_specs, out_specs=out_specs, check_vma=False)
```

time: 30.1 us -> 27.4 us (0.910)
  the two profiles are of different devices: /device:TPU:192 before, /device:TPU:65 now
where the time goes in v2:
time: 27.4 us; the launch traced here: 27 us
  Pallas kernels  26.3 us (96%)
  between operations  0.64 us (2%)
    pallas_call x1, Pallas kernels, local(): pl.pallas_call(exchange_kernel, out_shape=[pltpu.VMEM(shape, F32) for sha...  22.7 us
    pallas_call x1, Pallas kernels, local(): pl.pallas_call(store_kernel, out_shape=[jax.ShapeDtypeStruct(shape, F32)...  3.68 us

profile of v2, /device:TPU:65, one launch (start us, length us, event | category | flops | bytes accessed | tf_op | source)
XLA Modules:
  0.0 27.0 jit_solution(16130065446924690988)
XLA Ops:
  0.6 22.7 %exchange.1 = (f32[256,2048]{1,0:T(8,128)S(1)}, f32[2,256,2048]{2,1,0:T(8,128)S(1)}, f32[256,2048]{1,0:T(8,128)S(1)}, f32[2,18,64,128]{3,2,1,0:T(8,128)S(1)}, f3...) custom-call(f32[256,2048]{1,0:T(8,128)} %x.1), custom_call_target="tpu_custom_call" | custom-call | tf_op jit(solution)/shard_map/exchange/pallas_call | solution.py:495
  23.3 3.7 %store.1 = (f32[256,2048]{1,0:T(8,128)}, f32[2,256,2048]{2,1,0:T(8,128)}, f32[256,2048]{1,0:T(8,128)}) custom-call(f32[256,2048]{1,0:T(8,128)S(1)} %get-tuple-element.11.i_s, f32[2,256,2048]{2,1,0:T(8,128)S(1)} %get-tuple-element.12.i_f, f32[256,2048]{1,0:T(8,128)S(1)} %get-tuple-element.13.i_h, f32[2,18,64,128]{3,2,1,0:T(8,128)S(1)} %get-tuple-element.14.hz, ...), custom_call_target="tpu_custom_call" | custom-call | tf_op jit(solution)/shard_map/store/pallas_call | solution.py:517

commit v3 on v2

--- a/solution.py
+++ b/solution.py
@@ -141,15 +141,13 @@
     east, west = lax.rem(lon + 1, n_lon), lax.rem(lon + n_lon - 1, n_lon)
     has_north, has_south = lat > 0, lat < n_lat - 1
 
-    def load(k, j):
+    def load(k, j, n):
         return pltpu.make_async_copy(
-            x.at[pl.ds(64 * k, 64), pl.ds(128 * j, 128)], zc.at[j + 1, pl.ds(64 * k, 64)], sem_in.at[k, j]
+            x.at[pl.ds(64 * k, 64), pl.ds(128 * j, 128)], zc.at[j + 1, pl.ds(64 * k, 64)], sem_in.at[n]
         )
 
-    rims = [load(k, j) for k in (0, 3) for j in range(TILES)]
-    middle = [load(k, j) for k in (1, 2) for j in range(TILES)]
-    for c in rims + middle:
-        c.start()
+    def loaded(tiles, rows, n):
+        pltpu.make_async_copy(zc.at[tiles, rows], zc.at[tiles, rows], sem_in.at[n]).wait()
 
     barrier = pltpu.get_barrier_semaphore()
 
@@ -171,18 +169,29 @@
         for to in (lon, east, west):
             greet(lat + 1, to)
 
+    for n, (at, count) in enumerate(SPANS):
+        for j in range(at, at + count):
+            load(0, j, 2 * n).start()
+            load(3, j, 2 * n + 1).start()
+    for j in range(TILES):
+        load(1, j, 2 * len(SPANS)).start()
+        load(2, j, 2 * len(SPANS)).start()
+
     total_rows, total_cols = ROWS * n_lat, COLS * n_lon
     position = (lat * ROWS + lax.broadcasted_iota(jnp.int32, (ROWS, 128), 0)).astype(F32)
     spacing = jnp.sin((position + 0.5) * (math.pi / total_rows)) * (2.0 * total_rows / total_cols)
     gs[...] = 1.0 / (56.0 * spacing)
-    for c in rims:
-        c.wait()
-
-    def send(src, dst, k, to_lat, to_lon):
+
+    def rim_loaded(n):
+        at, count = SPANS[n]
+        loaded(pl.ds(1 + at, count), pl.ds(0, 64), 2 * n)
+        loaded(pl.ds(1 + at, count), pl.ds(192, 64), 2 * n + 1)
+
+    def send(src, dst, group, k, to_lat, to_lon):
         return pltpu.make_async_remote_copy(
             src_ref=src,
             dst_ref=dst,
-            send_sem=sem_out.at[k],
+            send_sem=sem_out.at[group],
             recv_sem=sem_got.at[k],
             device_id={"lat": to_lat, "lon": to_lon},
             device_id_type=pl.DeviceIdType.MESH,
@@ -191,35 +200,97 @@
     south, north = [], []
     for k, (at, n) in enumerate(SPANS):
         tiles = pl.ds(1 + at, n)
-        south.append(send(zc.at[tiles, pl.ds(192, 64)], hz.at[0, tiles], 6 + k, lat + 1, lon))
-        north.append(send(zc.at[tiles, pl.ds(0, 64)], hz.at[1, tiles], 10 + k, lat - 1, lon))
-    along = [send(packed.at[0], arrived.at[0], 0, lat, east), send(packed.at[1], arrived.at[1], 1, lat, west)]
+        south.append(send(zc.at[tiles, pl.ds(192, 64)], hz.at[0, tiles], 0, k, lat + 1, lon))
+        north.append(send(zc.at[tiles, pl.ds(0, 64)], hz.at[1, tiles], 1, 4 + k, lat - 1, lon))
+    along = [send(packed.at[0], arrived.at[0], 2, 8, lat, east), send(packed.at[1], arrived.at[1], 2, 8, lat, west)]
     top, bottom = pl.ds(0, 32), pl.ds(96, 32)
     south_corners = [
-        send(packed.at[0, bottom], corners.at[0, 0], 2, lat + 1, east),
-        send(packed.at[1, bottom], corners.at[0, 1], 3, lat + 1, west),
+        send(packed.at[0, bottom], corners.at[0, 0], 3, 9, lat + 1, east),
+        send(packed.at[1, bottom], corners.at[0, 1], 3, 9, lat + 1, west),
     ]
     north_corners = [
-        send(packed.at[0, top], corners.at[1, 0], 4, lat - 1, east),
-        send(packed.at[1, top], corners.at[1, 1], 5, lat - 1, west),
+        send(packed.at[0, top], corners.at[1, 0], 4, 10, lat - 1, east),
+        send(packed.at[1, top], corners.at[1, 1], 4, 10, lat - 1, west),
     ]
 
+    all_tiles = pl.ds(1, TILES)
+    all_south = send(zc.at[all_tiles, pl.ds(192, 64)], hz.at[0, all_tiles], 0, 0, lat + 1, lon)
+    all_north = send(zc.at[all_tiles, pl.ds(0, 64)], hz.at[1, all_tiles], 1, 4, lat - 1, lon)
+    all_along = send(packed, arrived, 2, 8, lat, east)
+    all_south_corners = send(packed.at[:, bottom], corners.at[0], 3, 9, lat + 1, east)
+    all_north_corners = send(packed.at[:, top], corners.at[1], 4, 10, lat - 1, east)
     inside = jnp.logical_and(has_north, has_south)
     pl.semaphore_wait(barrier, jnp.where(inside, 8, 5))
-    for k in range(len(SPANS)):
-        for c, there in ((south[k], has_south), (north[k], has_north)):
-
-            @pl.when(there)
-            def _(c=c):
-                c.start()
-
-    for c in middle:
-        c.wait()
+    rim_loaded(0)
+    @pl.when(has_south)
+    def _():
+        for c in south[0:1]:
+            c.start()
+
+    @pl.when(has_north)
+    def _():
+        for c in north[0:1]:
+            c.start()
+
+    rim_loaded(1)
+    @pl.when(has_south)
+    def _():
+        for c in south[1:2]:
+            c.start()
+
+    @pl.when(has_north)
+    def _():
+        for c in north[1:2]:
+            c.start()
+
+    rim_loaded(2)
+    @pl.when(has_south)
+    def _():
+        for c in south[2:3]:
+            c.start()
+
+    @pl.when(has_north)
+    def _():
+        for c in north[2:3]:
+            c.start()
+
+    rim_loaded(3)
+    @pl.when(has_south)
+    def _():
+        for c in south[3:4]:
+            c.start()
+
+    @pl.when(has_north)
+    def _():
+        for c in north[3:4]:
+            c.start()
+
+    loaded(pl.ds(1, TILES), pl.ds(64, 128), 2 * len(SPANS))
     low = lax.broadcasted_iota(jnp.int32, (32, 128), 1) < 64
     for k in range(4):
         one, two, to = slice(64 * k, 64 * k + 32), slice(64 * k + 32, 64 * k + 64), slice(32 * k, 32 * k + 32)
         packed[0, to, :] = jnp.where(low, pltpu.roll(zc[TILES, one, :], 64, 1), zc[TILES, two, :])
         packed[1, to, :] = jnp.where(low, zc[1, one, :], pltpu.roll(zc[1, two, :], 64, 1))
+
+    odd = lax.rem(lon, 2) == 1
+
+    @pl.when(jnp.logical_not(odd))
+    def _():
+        along[1].start()
+
+    @pl.when(odd)
+    def _():
+        along[0].start()
+
+    @pl.when(has_south)
+    def _():
+        for c in south_corners:
+            c.start()
+
+    @pl.when(has_north)
+    def _():
+        for c in north_corners:
+            c.start()
 
     for j in (0, TILES + 1):
         zc[j] = jnp.zeros((ROWS, 128), F32)
@@ -230,18 +301,13 @@
             ref[:, m + ROWS : m + ROWS + m, :] = jnp.zeros((TILES, m, 128), F32)
     clear(pt, qt)
 
-    for c in along:
-        c.start()
-
-    @pl.when(has_south)
-    def _():
-        for c in south_corners:
-            c.start()
-
-    @pl.when(has_north)
-    def _():
-        for c in north_corners:
-            c.start()
+    @pl.when(odd)
+    def _():
+        along[1].start()
+
+    @pl.when(jnp.logical_not(odd))
+    def _():
+        along[0].start()
 
     def first(row):
         for j, d in differences(lambda j: zc[j, pl.ds(row, 8), :], TILES, LAGS):
@@ -335,26 +401,23 @@
                     rows = slice(8 * g + 192 * side, 8 * g + 192 * side + 8)
                     put(rows, at + j, shade(*sums, gs[rows, :]))
 
-    for c in along:
-        c.wait()
-
-    @pl.when(has_south)
-    def _():
-        for c in north_corners:
-            c.wait_recv()
-        for c in south + south_corners:
-            c.wait_send()
-
-    @pl.when(has_north)
-    def _():
-        for c in south_corners:
-            c.wait_recv()
-        for c in north + north_corners:
-            c.wait_send()
+    all_along.wait()
+
+    @pl.when(has_south)
+    def _():
+        all_north_corners.wait_recv()
+        all_south.wait_send()
+        all_south_corners.wait_send()
+
+    @pl.when(has_north)
+    def _():
+        all_south_corners.wait_recv()
+        all_north.wait_send()
+        all_north_corners.wait_send()
 
 
 def store_kernel(
-    i_s, i_f, i_h, hz, ends, gs, arrived, corners, o_s, o_f, o_h, hc, outer, pt, qt, stage, sem, sem_ends
+    i_s, i_f, i_h, hz, ends, gs, arrived, corners, o_s, o_f, o_h, hc, outer, pt, qt, stage, sem
 ):
     lat, n_lat = lax.axis_index("lat"), lax.axis_size("lat")
 
@@ -366,12 +429,10 @@
             (i_h.at[at], o_h.at[at]),
         )
 
-    copies = []
+    of = (0, 1, 1, 2)
     for k in range(4):
         for n, (src, dst) in enumerate(pieces((pl.ds(64 * k, 64), pl.ds(128, COLS - 256)))):
-            copies.append(pltpu.make_async_copy(src, dst, sem.at[n, k]))
-    for c in copies:
-        c.start()
+            pltpu.make_async_copy(src, dst, sem.at[of[n]]).start()
 
     clear(pt, qt)
     for k, s in enumerate(LAGS):
@@ -450,9 +511,7 @@
             for e in range(2):
                 at = (pl.ds(64 * k, 64), pl.ds(128 * ENDS[e], 128))
                 dst = (o_s.at[at], o_f.at[(0, *at)], o_f.at[(1, *at)], o_h.at[at])[n]
-                c = pltpu.make_async_copy(stage.at[n, e, pl.ds(64 * k, 64)], dst, sem_ends.at[n, e, k])
-                c.start()
-                copies.append(c)
+                pltpu.make_async_copy(stage.at[n, e, pl.ds(64 * k, 64)], dst, sem.at[of[n]]).start()
 
     def middle(row):
         for r in range(4):
@@ -470,8 +529,8 @@
                 both = halo_sums(side, g, e, pt, qt, *sums(row, e))
                 put(row, e, shade(*both, gs[row : row + 8, :]))
         flush(3 * side)
-    for c in copies:
-        c.wait()
+    for n, (src, dst) in enumerate(((i_s, o_s), (i_f, o_f), (i_h, o_h))):
+        pltpu.make_async_copy(src, dst, sem.at[n]).wait()
 
 
 OUTPUTS = ((ROWS, COLS), (2, ROWS, COLS), (ROWS, COLS))
@@ -506,9 +565,9 @@
             pltpu.VMEM((2, 2, TILES, HALO, 128), F32),
             near(MOST),
             near(MOST),
-            pltpu.SemaphoreType.DMA((4, TILES)),
-            pltpu.SemaphoreType.DMA((14,)),
-            pltpu.SemaphoreType.DMA((14,)),
+            pltpu.SemaphoreType.DMA((2 * len(SPANS) + 1,)),
+            pltpu.SemaphoreType.DMA((5,)),
+            pltpu.SemaphoreType.DMA((11,)),
         ],
         compiler_params=pltpu.CompilerParams(collective_id=0, has_side_effects=True, vmem_limit_bytes=46 << 20),
         name="exchange",
@@ -525,8 +584,7 @@
                 near(2),
                 near(2),
                 pltpu.VMEM((4, 2, ROWS, 128), F32),
-                pltpu.SemaphoreType.DMA((4, 4)),
-                pltpu.SemaphoreType.DMA((4, 2, 4)),
+                pltpu.SemaphoreType.DMA((3,)),
             ],
             compiler_params=pltpu.CompilerParams(vmem_limit_bytes=16 << 20),
             name="store",

time: 27.4 us -> 26.3 us (0.960)
  Pallas kernels: 26.3 us -> 25.3 us
    pallas_call x1, Pallas kernels: 22.7 us -> 22 us  [local(): pl.pallas_call(exchange_kernel, out_shape=[pltpu.VMEM(shape, F32) for sha...]
    pallas_call x1, Pallas kernels: 3.68 us -> 3.27 us  [local(): pl.pallas_call(store_kernel, out_shape=[jax.ShapeDtypeStruct(shape, F32)...]
where the time goes in v3:
time: 26.3 us; the launch traced here: 25.9 us
  Pallas kernels  25.3 us (96%)
  between operations  0.64 us (2%)
    pallas_call x1, Pallas kernels, local(): pl.pallas_call(exchange_kernel, out_shape=[pltpu.VMEM(shape, F32) for sha...  22 us
    pallas_call x1, Pallas kernels, local(): pl.pallas_call(store_kernel, out_shape=[jax.ShapeDtypeStruct(shape, F32)...  3.27 us

profile of v3, /device:TPU:65, one launch (start us, length us, event | category | flops | bytes accessed | tf_op | source)
XLA Modules:
  0.0 25.9 jit_solution(2053744069564990415)
XLA Ops:
  0.6 22.0 %exchange.1 = (f32[256,2048]{1,0:T(8,128)S(1)}, f32[2,256,2048]{2,1,0:T(8,128)S(1)}, f32[256,2048]{1,0:T(8,128)S(1)}, f32[2,18,64,128]{3,2,1,0:T(8,128)S(1)}, f3...) custom-call(f32[256,2048]{1,0:T(8,128)} %x.1), custom_call_target="tpu_custom_call" | custom-call | tf_op jit(solution)/shard_map/exchange/pallas_call | solution.py:554
  22.6 3.3 %store.1 = (f32[256,2048]{1,0:T(8,128)}, f32[2,256,2048]{2,1,0:T(8,128)}, f32[256,2048]{1,0:T(8,128)}) custom-call(f32[256,2048]{1,0:T(8,128)S(1)} %get-tuple-element.11.i_s, f32[2,256,2048]{2,1,0:T(8,128)S(1)} %get-tuple-element.12.i_f, f32[256,2048]{1,0:T(8,128)S(1)} %get-tuple-element.13.i_h, f32[2,18,64,128]{3,2,1,0:T(8,128)S(1)} %get-tuple-element.14.hz, ...), custom_call_target="tpu_custom_call" | custom-call | tf_op jit(solution)/shard_map/store/pallas_call | solution.py:576

commit v4 on v3

--- a/solution.py
+++ b/solution.py
@@ -220,51 +220,10 @@
     all_south_corners = send(packed.at[:, bottom], corners.at[0], 3, 9, lat + 1, east)
     all_north_corners = send(packed.at[:, top], corners.at[1], 4, 10, lat - 1, east)
     inside = jnp.logical_and(has_north, has_south)
-    pl.semaphore_wait(barrier, jnp.where(inside, 8, 5))
     rim_loaded(0)
-    @pl.when(has_south)
-    def _():
-        for c in south[0:1]:
-            c.start()
-
-    @pl.when(has_north)
-    def _():
-        for c in north[0:1]:
-            c.start()
-
     rim_loaded(1)
-    @pl.when(has_south)
-    def _():
-        for c in south[1:2]:
-            c.start()
-
-    @pl.when(has_north)
-    def _():
-        for c in north[1:2]:
-            c.start()
-
     rim_loaded(2)
-    @pl.when(has_south)
-    def _():
-        for c in south[2:3]:
-            c.start()
-
-    @pl.when(has_north)
-    def _():
-        for c in north[2:3]:
-            c.start()
-
     rim_loaded(3)
-    @pl.when(has_south)
-    def _():
-        for c in south[3:4]:
-            c.start()
-
-    @pl.when(has_north)
-    def _():
-        for c in north[3:4]:
-            c.start()
-
     loaded(pl.ds(1, TILES), pl.ds(64, 128), 2 * len(SPANS))
     low = lax.broadcasted_iota(jnp.int32, (32, 128), 1) < 64
     for k in range(4):
@@ -272,24 +231,64 @@
         packed[0, to, :] = jnp.where(low, pltpu.roll(zc[TILES, one, :], 64, 1), zc[TILES, two, :])
         packed[1, to, :] = jnp.where(low, zc[1, one, :], pltpu.roll(zc[1, two, :], 64, 1))
 
+    pl.semaphore_wait(barrier, jnp.where(inside, 8, 5))
     odd = lax.rem(lon, 2) == 1
 
-    @pl.when(jnp.logical_not(odd))
-    def _():
-        along[1].start()
-
-    @pl.when(odd)
-    def _():
-        along[0].start()
-
+    def start_rest(now):
+        def begin(when, *group):
+            @pl.when(jnp.logical_and(now, when))
+            def _():
+                for c in group:
+                    c.start()
+
+        begin(jnp.logical_not(odd), along[1])
+        begin(odd, along[0])
+        begin(has_south, *south_corners)
+        begin(has_north, *north_corners)
+        begin(odd, along[1])
+        begin(jnp.logical_not(odd), along[0])
+
+    quarter = lax.rem(lat, 4)
+    level = jnp.logical_or(quarter == 1, quarter == 2)
+    start_rest(jnp.logical_not(level))
     @pl.when(has_south)
     def _():
-        for c in south_corners:
+        for c in south[0:1]:
             c.start()
 
     @pl.when(has_north)
     def _():
-        for c in north_corners:
+        for c in north[0:1]:
+            c.start()
+
+    @pl.when(has_south)
+    def _():
+        for c in south[1:2]:
+            c.start()
+
+    @pl.when(has_north)
+    def _():
+        for c in north[1:2]:
+            c.start()
+
+    @pl.when(has_south)
+    def _():
+        for c in south[2:3]:
+            c.start()
+
+    @pl.when(has_north)
+    def _():
+        for c in north[2:3]:
+            c.start()
+
+    @pl.when(has_south)
+    def _():
+        for c in south[3:4]:
+            c.start()
+
+    @pl.when(has_north)
+    def _():
+        for c in north[3:4]:
             c.start()
 
     for j in (0, TILES + 1):
@@ -301,13 +300,7 @@
             ref[:, m + ROWS : m + ROWS + m, :] = jnp.zeros((TILES, m, 128), F32)
     clear(pt, qt)
 
-    @pl.when(odd)
-    def _():
-        along[1].start()
-
-    @pl.when(jnp.logical_not(odd))
-    def _():
-        along[0].start()
+    start_rest(level)
 
     def first(row):
         for j, d in differences(lambda j: zc[j, pl.ds(row, 8), :], TILES, LAGS):

time: 26.3 us -> 26.1 us (level)
  no operation moved by 1% of the time
where the time goes in v4:
time: 26.1 us; the launch traced here: 25.9 us
  Pallas kernels  25.3 us (97%)
  between operations  0.64 us (2%)
    pallas_call x1, Pallas kernels, local(): pl.pallas_call(exchange_kernel, out_shape=[pltpu.VMEM(shape, F32) for sha...  22 us
    pallas_call x1, Pallas kernels, local(): pl.pallas_call(store_kernel, out_shape=[jax.ShapeDtypeStruct(shape, F32)...  3.27 us

profile of v4, /device:TPU:65, one launch (start us, length us, event | category | flops | bytes accessed | tf_op | source)
XLA Modules:
  0.0 25.9 jit_solution(7643020741895650386)
XLA Ops:
  0.6 22.0 %exchange.1 = (f32[256,2048]{1,0:T(8,128)S(1)}, f32[2,256,2048]{2,1,0:T(8,128)S(1)}, f32[256,2048]{1,0:T(8,128)S(1)}, f32[2,18,64,128]{3,2,1,0:T(8,128)S(1)}, f3...) custom-call(f32[256,2048]{1,0:T(8,128)} %x.1), custom_call_target="tpu_custom_call" | custom-call | tf_op jit(solution)/shard_map/exchange/pallas_call | solution.py:547
  22.6 3.3 %store.1 = (f32[256,2048]{1,0:T(8,128)}, f32[2,256,2048]{2,1,0:T(8,128)}, f32[256,2048]{1,0:T(8,128)}) custom-call(f32[256,2048]{1,0:T(8,128)S(1)} %get-tuple-element.11.i_s, f32[2,256,2048]{2,1,0:T(8,128)S(1)} %get-tuple-element.12.i_f, f32[256,2048]{1,0:T(8,128)S(1)} %get-tuple-element.13.i_h, f32[2,18,64,128]{3,2,1,0:T(8,128)S(1)} %get-tuple-element.14.hz, ...), custom_call_target="tpu_custom_call" | custom-call | tf_op jit(solution)/shard_map/store/pallas_call | solution.py:569
